TPU v7x, 32 devices: a whole 2x2x4 slice. The times are simulated.
32 devices in a mesh: owner: 8 (over z, y), rows: 4 (over x, core).
Axes of the slice: x: 2, y: 2, z: 4, core: 2. Of those that a mesh axis runs over, the one named last changes fastest.
Arguments:
- master_down: float32 [16, 6400, 4096], P('owner', None, 'rows'), may hold values from -0.109375 to 0.109375
- router_weight: float32 [4096, 16], P('rows', 'owner'), may hold values from -0.09375 to 0.09375
- router_gain: float32 [4096], P('rows'), may hold values from 0.25 to 1.75
Outputs:
- final_down: bfloat16 [16, 6400, 4096], P('owner', 'rows')
- scale_down: float32 [16, 6400], P('owner', 'rows')
- serve_router: bfloat16 [4096, 16], replicated
All inputs are finite; a program needn't handle non-finite values. Where the computation divides by a largest or mean magnitude, that divisor is 1e-20 or more.
Results may differ from a plain program's by a relative error of at most 0.001.
Values may be sent and summed in bfloat16 or wider, within the bound.
A program may use at most 192 MiB of HBM per device.

v0:
```python
import jax
import jax.numpy as jnp
from jax import lax
from jax.sharding import PartitionSpec as P

D_MODEL = 4096


def per_device(master_down, router_weight, router_gain):
    total_down = lax.psum(jnp.sum(jnp.abs(master_down), axis=2), "rows")
    scale_down = total_down / D_MODEL
    narrow_down = (master_down / jnp.expand_dims(scale_down, 2)).astype(jnp.bfloat16)
    final_down = lax.all_to_all(narrow_down, "rows", split_axis=1, concat_axis=2, tiled=True)
    scale_down = lax.dynamic_slice_in_dim(
        scale_down, lax.axis_index("rows") * final_down.shape[1], final_down.shape[1], axis=1
    )
    part_router = (router_weight * router_gain[:, None]).astype(jnp.bfloat16)
    row_router = lax.all_gather(part_router, "rows", axis=0, tiled=True)
    serve_router = lax.all_gather(row_router, "owner", axis=1, tiled=True)
    return (final_down, scale_down, serve_router)


def solution(mesh):
    return jax.shard_map(
        per_device,
        mesh=mesh,
        in_specs=(P("owner", None, "rows"), P("rows", "owner"), P("rows")),
        out_specs=(P("owner", "rows", None), P("owner", "rows"), P()),
        check_vma=False,
    )
```

profile of v0, /device:TPU:0, one launch (start us, length us, event | category | flops | bytes accessed | tf_op | source)
XLA Modules:
  0.0 506.3 jit_solution(15090514093543817720)
XLA Ops:
  0.6 17.0 %abs_reduce_fusion = f32[2,6400]{1,0:T(2,128)S(1)} fusion(f32[2,6400,1024]{2,1,0:T(8,128)} %param.3), kind=kLoop, calls=%fused_computation.1 | loop fusion | flops 26201600 | bytes 52480000 | tf_op jit(solution)/shard_map/reduce_sum | solution.py:10
  17.6 13.4 %psum.7 = f32[2,6400]{1,0:T(2,128)S(1)} all-reduce(f32[2,6400]{1,0:T(2,128)S(1)} %abs_reduce_fusion), channel_id=1, replica_groups=mesh['owner'=8,'rows'=4] {'rows'}, use_global_device_ids=true, to_apply=%region_1.0 | all-reduce | flops 12800 | bytes 102400 | tf_op jit(solution)/shard_map/psum | solution.py:10
  31.1 26.1 %divide_convert_fusion = bf16[2,6400,1024]{2,1,0:T(8,128)(2,1)} fusion(f32[2,6400,1024]{2,1,0:T(8,128)} %param.3, f32[2,6400]{1,0:T(2,128)S(1)} %broadcast_multiply_fusion), kind=kLoop, calls=%fused_computation | loop fusion | flops 26214400 | bytes 78694400 | tf_op jit(solution)/shard_map/convert_element_type | solution.py:12
  57.2 0.0 copy-start
  57.2 0.0 copy-start.1
  57.2 47.4 %copy.10 = bf16[2,6400,1024]{2,0,1:T(2,128)(2,1)} copy(bf16[2,6400,1024]{2,1,0:T(8,128)(2,1)} %divide_convert_fusion) | data formatting | bytes 52428800 | tf_op jit(solution)/shard_map/convert_element_type | solution.py:12
  104.6 8.6 %all-to-all-start = ((bf16[2,6400,1024]{2,0,1:T(2,128)(2,1)}), bf16[2,6400,1024]{2,0,1:T(2,128)(2,1)}, u32[]{:S(2)}, u32[]{:S(2)}) async-start(bf16[2,6400,1024]{2,0,1:T(2,128)(2,1)} %copy.10), calls=%async_computation | async-start | bytes 52428800 | tf_op jit(solution)/shard_map/all_to_all | solution.py:13
  113.2 0.0 copy-done
  113.2 0.0 copy-done.1
  113.2 285.0 %all_gather.6 = bf16[4096,2]{0,1:T(2,128)(2,1)S(1)} all-gather(bf16[1024,2]{0,1:T(2,128)(2,1)S(1)} %multiply_convert_fusion), channel_id=1, replica_groups=mesh['owner'=8,'rows'=4] {'rows'}, dimensions={0}, use_global_device_ids=true | all-gather | bytes 20480 | tf_op jit(solution)/shard_map/all_gather | solution.py:18
  398.2 30.9 %all-gather = bf16[8,2,4096]{2,1,0:T(2,128)(2,1)S(1)} all-gather(bf16[1,2,4096]{2,1,0:T(2,128)(2,1)S(1)} %bitcast.8), channel_id=1, replica_groups=mesh['owner'=8,'rows'=4] {'owner'}, dimensions={0}, use_global_device_ids=true | all-gather | bytes 147456 | tf_op jit(solution)/shard_map/all_gather | solution.py:19
  429.1 0.7 reshape.9
  429.8 0.7 constant_dynamic-slice_fusion
  430.5 0.0 all-to-all-done
  430.5 33.4 %copy.11 = bf16[2,1600,4,1024]{3,2,1,0:T(4,128)(2,1)} copy(bf16[2,1600,4,1024]{3,0,1,2:T(2,128)(2,1)} %bitcast.1) | data formatting | bytes 52428800 | tf_op jit(solution)/shard_map/all_to_all | solution.py:13
  463.9 42.5 %all_to_all.16 = bf16[2,1600,4096]{2,1,0:T(8,128)(2,1)} reshape(bf16[2,1600,4,1024]{3,2,1,0:T(4,128)(2,1)} %copy.11) | data formatting | bytes 52428800 | tf_op jit(solution)/shard_map/all_to_all | solution.py:13
  (2 shorter events, 0.0 us)
Async XLA Ops:
  57.2 56.0 %copy-start = (f32[1024,2]{0,1:T(2,128)S(1)}, f32[1024,2]{0,1:T(2,128)}, u32[]{:S(2)}) copy-start(f32[1024,2]{0,1:T(2,128)} %param.4) | copy-start | bytes 24580
  57.2 56.0 %copy-start.1 = (f32[1024]{0:T(1024)S(1)}, f32[1024]{0:T(1024)}, u32[]{:S(2)}) copy-start(f32[1024]{0:T(1024)} %param.5) | copy-start | bytes 12292
  104.6 325.9 %all-to-all-start = ((bf16[2,6400,1024]{2,0,1:T(2,128)(2,1)}), bf16[2,6400,1024]{2,0,1:T(2,128)(2,1)}, u32[]{:S(2)}, u32[]{:S(2)}) async-start(bf16[2,6400,1024]{2,0,1:T(2,128)(2,1)} %copy.10), calls=%async_computation | async-start | bytes 52428800 | tf_op jit(solution)/shard_map/all_to_all | solution.py:13
where the time goes:
time: 508 us; the launch traced here: 506 us
  blocking collectives  329 us (65%)
  local copies, waits for them, and re-layouts  125 us (25%)
  other arithmetic  43.2 us (9%)
  starting transfers between devices  8.59 us (2%)
    all_gather x1, blocking collectives, per_device(): row_router = lax.all_gather(part_router, 'rows', axis=0, tiled=True)  285 us
    all_to_all x2, local copies, waits for them, and re-layouts, per_device(): lax.all_to_all(narrow_down, 'rows', split_axis=1, concat_axis=2, tiled=True)  75.8 us
    convert_element_type x1, local copies, waits for them, and re-layouts, per_device(): (master_down / jnp.expand_dims(scale_down, 2)).astype(jnp.bfloat16)  47.4 us
    all_gather x1, blocking collectives, per_device(): serve_router = lax.all_gather(row_router, 'owner', axis=1, tiled=True)  30.9 us
    convert_element_type x1, other arithmetic, per_device(): (master_down / jnp.expand_dims(scale_down, 2)).astype(jnp.bfloat16)  26.1 us
    reduce_sum x1, other arithmetic, per_device(): total_down = lax.psum(jnp.sum(jnp.abs(master_down), axis=2), 'rows')  17 us
    psum x1, blocking collectives, per_device(): total_down = lax.psum(jnp.sum(jnp.abs(master_down), axis=2), 'rows')  13.4 us
  transfers between devices with their start and end apart: 1, of which 0 were waited for; matrix products, arithmetic and copies ran while one was open for 0% of the time, Pallas kernels for 0%

commit v1 on v0

--- a/solution.py
+++ b/solution.py
@@ -16,7 +16,7 @@
     )
     part_router = (router_weight * router_gain[:, None]).astype(jnp.bfloat16)
     row_router = lax.all_gather(part_router, "rows", axis=0, tiled=True)
-    serve_router = lax.all_gather(row_router, "owner", axis=1, tiled=True)
+    serve_router = jnp.concatenate(lax.all_gather(row_router, "owner"), axis=1)
     return (final_down, scale_down, serve_router)
 
 

time: 508 us -> 508 us (level)
  no operation moved by 1% of the time
where the time goes in v1:
time: 508 us; the launch traced here: 506 us
  blocking collectives  329 us (65%)
  local copies, waits for them, and re-layouts  125 us (25%)
  other arithmetic  43.2 us (9%)
  starting transfers between devices  8.59 us (2%)
    all_gather x1, blocking collectives, per_device(): row_router = lax.all_gather(part_router, 'rows', axis=0, tiled=True)  285 us
    all_to_all x2, local copies, waits for them, and re-layouts, per_device(): lax.all_to_all(narrow_down, 'rows', split_axis=1, concat_axis=2, tiled=True)  75.8 us
    convert_element_type x1, local copies, waits for them, and re-layouts, per_device(): (master_down / jnp.expand_dims(scale_down, 2)).astype(jnp.bfloat16)  47.4 us
    all_gather x1, blocking collectives, per_device(): serve_router = jnp.concatenate(lax.all_gather(row_router, 'owner'), axis=1)  30.9 us
    convert_element_type x1, other arithmetic, per_device(): (master_down / jnp.expand_dims(scale_down, 2)).astype(jnp.bfloat16)  26.1 us
    reduce_sum x1, other arithmetic, per_device(): total_down = lax.psum(jnp.sum(jnp.abs(master_down), axis=2), 'rows')  17 us
    psum x1, blocking collectives, per_device(): total_down = lax.psum(jnp.sum(jnp.abs(master_down), axis=2), 'rows')  13.4 us
  transfers between devices with their start and end apart: 1, of which 0 were waited for; matrix products, arithmetic and copies ran while one was open for 0% of the time, Pallas kernels for 0%

profile of v1, /device:TPU:0, one launch (start us, length us, event | category | flops | bytes accessed | tf_op | source)
XLA Modules:
  0.0 506.3 jit_solution(16051430214802116243)
XLA Ops:
  0.6 17.0 %abs_reduce_fusion = f32[2,6400]{1,0:T(2,128)S(1)} fusion(f32[2,6400,1024]{2,1,0:T(8,128)} %param.3), kind=kLoop, calls=%fused_computation.1 | loop fusion | flops 26201600 | bytes 52480000 | tf_op jit(solution)/shard_map/reduce_sum | solution.py:10
  17.6 13.4 %psum.7 = f32[2,6400]{1,0:T(2,128)S(1)} all-reduce(f32[2,6400]{1,0:T(2,128)S(1)} %abs_reduce_fusion), channel_id=1, replica_groups=mesh['owner'=8,'rows'=4] {'rows'}, use_global_device_ids=true, to_apply=%region_1.0 | all-reduce | flops 12800 | bytes 102400 | tf_op jit(solution)/shard_map/psum | solution.py:10
  31.1 26.1 %divide_convert_fusion = bf16[2,6400,1024]{2,1,0:T(8,128)(2,1)} fusion(f32[2,6400,1024]{2,1,0:T(8,128)} %param.3, f32[2,6400]{1,0:T(2,128)S(1)} %broadcast_multiply_fusion), kind=kLoop, calls=%fused_computation | loop fusion | flops 26214400 | bytes 78694400 | tf_op jit(solution)/shard_map/convert_element_type | solution.py:12
  57.2 0.0 copy-start
  57.2 0.0 copy-start.1
  57.2 47.4 %copy.12 = bf16[2,6400,1024]{2,0,1:T(2,128)(2,1)} copy(bf16[2,6400,1024]{2,1,0:T(8,128)(2,1)} %divide_convert_fusion) | data formatting | bytes 52428800 | tf_op jit(solution)/shard_map/convert_element_type | solution.py:12
  104.6 8.6 %all-to-all-start = ((bf16[2,6400,1024]{2,0,1:T(2,128)(2,1)}), bf16[2,6400,1024]{2,0,1:T(2,128)(2,1)}, u32[]{:S(2)}, u32[]{:S(2)}) async-start(bf16[2,6400,1024]{2,0,1:T(2,128)(2,1)} %copy.12), calls=%async_computation | async-start | bytes 52428800 | tf_op jit(solution)/shard_map/all_to_all | solution.py:13
  113.2 0.0 copy-done
  113.2 0.0 copy-done.1
  113.2 285.0 %all_gather.9 = bf16[4096,2]{0,1:T(2,128)(2,1)S(1)} all-gather(bf16[1024,2]{0,1:T(2,128)(2,1)S(1)} %multiply_convert_fusion), channel_id=1, replica_groups=mesh['owner'=8,'rows'=4] {'rows'}, dimensions={0}, use_global_device_ids=true | all-gather | bytes 20480 | tf_op jit(solution)/shard_map/all_gather | solution.py:18
  398.2 30.9 %all-gather = bf16[32768,2]{0,1:T(2,128)(2,1)S(1)} all-gather(bf16[4096,2]{0,1:T(2,128)(2,1)S(1)} %all_gather.9), channel_id=2, replica_groups=mesh['owner'=8,'rows'=4] {'owner'}, dimensions={0}, use_global_device_ids=true | all-gather | bytes 147456 | tf_op jit(solution)/shard_map/all_gather | solution.py:19
  429.1 0.7 reshape.15
  429.8 0.7 constant_dynamic-slice_fusion
  430.5 0.0 all-to-all-done
  430.5 33.4 %copy.13 = bf16[2,1600,4,1024]{3,2,1,0:T(4,128)(2,1)} copy(bf16[2,1600,4,1024]{3,0,1,2:T(2,128)(2,1)} %bitcast.1) | data formatting | bytes 52428800 | tf_op jit(solution)/shard_map/all_to_all | solution.py:13
  463.9 42.5 %all_to_all.16 = bf16[2,1600,4096]{2,1,0:T(8,128)(2,1)} reshape(bf16[2,1600,4,1024]{3,2,1,0:T(4,128)(2,1)} %copy.13) | data formatting | bytes 52428800 | tf_op jit(solution)/shard_map/all_to_all | solution.py:13
  (2 shorter events, 0.0 us)
Async XLA Ops:
  57.2 56.0 %copy-start = (f32[1024,2]{0,1:T(2,128)S(1)}, f32[1024,2]{0,1:T(2,128)}, u32[]{:S(2)}) copy-start(f32[1024,2]{0,1:T(2,128)} %param.4) | copy-start | bytes 24580
  57.2 56.0 %copy-start.1 = (f32[1024]{0:T(1024)S(1)}, f32[1024]{0:T(1024)}, u32[]{:S(2)}) copy-start(f32[1024]{0:T(1024)} %param.5) | copy-start | bytes 12292
  104.6 325.9 %all-to-all-start = ((bf16[2,6400,1024]{2,0,1:T(2,128)(2,1)}), bf16[2,6400,1024]{2,0,1:T(2,128)(2,1)}, u32[]{:S(2)}, u32[]{:S(2)}) async-start(bf16[2,6400,1024]{2,0,1:T(2,128)(2,1)} %copy.12), calls=%async_computation | async-start | bytes 52428800 | tf_op jit(solution)/shard_map/all_to_all | solution.py:13
